TPU v7x, 16 devices: a whole 2x2x2 slice. The times are simulated.
16 devices in a mesh: dp: 4 (over z, y), tp: 4 (over x, core).
Axes of the slice: x: 2, y: 2, z: 2, core: 2. Of those that a mesh axis runs over, the one named last changes fastest.
Arguments:
- tokens: int32 [4, 2048], P('dp')
- emb_table: bfloat16 [65536, 3072], P('tp')
- w_norm: float32 [3072], replicated
- dy_norm: bfloat16 [4, 2048, 3072], P('dp', 'tp')
- dy_resid: bfloat16 [4, 2048, 3072], P('dp', 'tp')
Outputs:
- output 1: bfloat16 [4, 2048, 3072], P('dp', 'tp')
- output 2: bfloat16 [4, 2048, 3072], P('dp', 'tp')
- output 3: float32 [65536, 3072], P(('tp', 'dp'))
- output 4: float32 [3072], replicated
All inputs are finite; a program needn't handle non-finite values.
Results may differ from a plain program's by a relative error of at most 0.00840549.
Values sent between devices are 32-bit elements.
A program may use at most 1 GiB of HBM per device.

v0:
```python
import functools
import math
import jax
import jax.numpy as jnp
import numpy as np
from jax import lax
from jax.sharding import PartitionSpec as P
from jax.experimental import pallas as pl
from jax.experimental.pallas import tpu as pltpu

NORM_EPS = 1e-6
MESH = pl.DeviceIdType.MESH
NDEV = 16
OWN_ROWS = 4096
CAPS = (1536, 576, 368, 368) + (288,) * 4 + (224,) * 8
HALF = tuple(c // 2 for c in CAPS)
HBASE = tuple(sum(HALF[:i]) for i in range(NDEV))
HTOT = sum(HALF)
CAPMAX = max(CAPS)
FAR_CAP = 640
FWD_CHUNKS = 2
ROW_TILE = 64
ACCS = 4
UNROLL = 4
TILE = 128


def coords():
    dp, tp = lax.axis_index("dp"), lax.axis_index("tp")
    return dp // 2, dp % 2, tp // 2, tp % 2


def peer(z, y, x, c, k):
    pz, py, px = (z + k // 4) % 2, (y + (k // 2) % 2) % 2, (x + k % 2) % 2
    dp, tp = pz * 2 + py, px * 2 + c
    return dp, tp, dp * 2 + px


def columns_kernel(g_ref, out_ref, stage, send, recv, fsend, frecv, lsem):
    z, y, x, c = coords()
    dp = z * 2 + y
    q = dp * 2 + x
    cols = out_ref.shape[2]
    partner = (dp, x * 2 + (1 - c))
    barrier = pltpu.get_barrier_semaphore()
    for k in range(1, 8):
        pdp, ptp, _ = peer(z, y, x, c, k)
        pl.semaphore_signal(barrier, inc=1, device_id=(pdp, ptp), device_id_type=MESH)
    pl.semaphore_signal(barrier, inc=1, device_id=partner, device_id_type=MESH)
    pl.semaphore_wait(barrier, 8)

    def block(qq):
        return g_ref.at[:, pl.ds(pl.multiple_of(qq * cols, 128), cols)]

    sends = []
    for k in (7, 3, 5, 6, 1, 2, 4):
        pdp, ptp, pq = peer(z, y, x, c, k)
        cp = pltpu.make_async_remote_copy(
            src_ref=block(pq), dst_ref=out_ref.at[q * 2 + c],
            send_sem=send.at[k], recv_sem=recv.at[k],
            device_id=(pdp, ptp), device_id_type=MESH)
        cp.start()
        sends.append((k, pq, cp))
    fwd = pltpu.make_async_remote_copy(
        src_ref=block(q), dst_ref=out_ref.at[q * 2 + c],
        send_sem=fsend.at[0], recv_sem=frecv.at[0],
        device_id=partner, device_id_type=MESH)
    fwd.start()
    forwards = [fwd]
    cin = pltpu.make_async_copy(block(q), stage, lsem.at[0])
    cin.start()
    cin.wait()
    cout = pltpu.make_async_copy(stage, out_ref.at[q * 2 + c], lsem.at[1])
    cout.start()
    for k, pq, cp in sorted(sends, key=lambda s: bin(s[0]).count("1")):
        cp.wait_recv()
        f = pltpu.make_async_remote_copy(
            src_ref=out_ref.at[pq * 2 + c], dst_ref=out_ref.at[pq * 2 + c],
            send_sem=fsend.at[k], recv_sem=frecv.at[k],
            device_id=partner, device_id_type=MESH)
        f.start()
        forwards.append(f)
    cout.wait()
    for k, pq, cp in sends:
        cp.wait_send()
    for f in forwards:
        f.wait()


def exchange_columns(g):
    rows, width = g.shape
    cols = width // 8
    return pl.pallas_call(
        columns_kernel,
        out_shape=jax.ShapeDtypeStruct((NDEV, rows, cols), g.dtype),
        in_specs=[pl.BlockSpec(memory_space=pl.ANY)],
        out_specs=pl.BlockSpec(memory_space=pl.ANY),
        scratch_shapes=[
            pltpu.VMEM((rows, cols), g.dtype),
            pltpu.SemaphoreType.DMA((8,)),
            pltpu.SemaphoreType.DMA((8,)),
            pltpu.SemaphoreType.DMA((8,)),
            pltpu.SemaphoreType.DMA((8,)),
            pltpu.SemaphoreType.DMA((2,)),
        ],
        compiler_params=pltpu.CompilerParams(collective_id=1, has_side_effects=True),
        name="exchange_columns",
    )(g)


def sum_kernel(rows, tok_rows, work_ref, count_ref, got_ref, acc_ref, *more):
    accs = (acc_ref,) + more
    lanes = len(accs)
    for ref in accs:
        ref[...] = jnp.zeros_like(ref)
    wsum = got_ref[pl.ds(tok_rows, 8), :]
    for s in range(1, NDEV):
        wsum = wsum + got_ref[pl.ds(s * rows + tok_rows, 8), :]
    n = count_ref[0]

    def group(base, refs):
        ws = [work_ref[base + u] for u in range(len(refs))]
        new = [got_ref[pl.ds(w >> 12, 1), :] for w in ws]
        old = [ref[pl.ds(w & 4095, 1), :] for ref, w in zip(refs, ws)]
        for ref, w, a, b in zip(refs, ws, old, new):
            ref[pl.ds(w & 4095, 1), :] = a + b

    def body(i, carry):
        for u in range(UNROLL):
            group((i * UNROLL + u) * lanes, accs)
        return carry

    step = UNROLL * lanes
    lax.fori_loop(0, n // step, body, 0)

    def tail(i, carry):
        group(i, accs[:1])
        return carry

    lax.fori_loop((n // step) * step, n, tail, 0)
    total = accs[0][...]
    for ref in more:
        total = total + ref[...]
    acc_ref[...] = total
    acc_ref[pl.ds(HTOT, 8), :] = wsum


def sum_duplicates(work, count, got, tok_rows):
    _, rows, cols = got.shape
    out_rows = HTOT + 8
    return pl.pallas_call(
        functools.partial(sum_kernel, rows, tok_rows),
        grid_spec=pltpu.PrefetchScalarGridSpec(
            num_scalar_prefetch=2, grid=(1,),
            in_specs=[pl.BlockSpec((NDEV * rows, cols), lambda i, *_: (0, 0))],
            out_specs=pl.BlockSpec((out_rows, cols), lambda i, *_: (0, 0)),
            scratch_shapes=[pltpu.VMEM((out_rows, cols), jnp.float32)] * (ACCS - 1),
        ),
        out_shape=jax.ShapeDtypeStruct((out_rows, cols), jnp.float32),
        compiler_params=pltpu.CompilerParams(vmem_limit_bytes=60 * 2**20),
        name="sum_duplicates",
    )(work, count, got.reshape(NDEV * rows, cols))


def owners_kernel(acc_ref, got_ref, w_ref, send, recv, wsend, wrecv, lsem):
    z, y, x, c = coords()
    dp, tp = z * 2 + y, x * 2 + c
    q = dp * 2 + x
    me = q * 2 + c
    own = tp * 4 + dp
    cols = acc_ref.shape[1]
    lanes = pl.ds(pl.multiple_of(q * cols, 128), cols)
    barrier = pltpu.get_barrier_semaphore()
    for d in range(NDEV):
        @pl.when(own != d)
        def _():
            pl.semaphore_signal(barrier, inc=1, device_id=(d % 4, d // 4), device_id_type=MESH)
    pl.semaphore_wait(barrier, NDEV - 1)

    def remote(d):
        h = HALF[d]
        return pltpu.make_async_remote_copy(
            src_ref=acc_ref.at[pl.ds(HBASE[d], h), :],
            dst_ref=got_ref.at[pl.ds(pl.multiple_of(c * h, 8), h), lanes],
            send_sem=send.at[d], recv_sem=recv.at[me],
            device_id=(d % 4, d // 4), device_id_type=MESH)

    def local(d):
        h = HALF[d]
        return pltpu.make_async_copy(
            acc_ref.at[pl.ds(HBASE[d], h), :],
            got_ref.at[pl.ds(pl.multiple_of(c * h, 8), h), lanes], lsem.at[0])

    wrow = acc_ref.at[pl.ds(HTOT, 8), :]

    def wcopy(k):
        pdp, ptp, _ = peer(z, y, x, c, k)
        return pltpu.make_async_remote_copy(
            src_ref=wrow, dst_ref=w_ref.at[:, lanes],
            send_sem=wsend.at[k], recv_sem=wrecv.at[k],
            device_id=(pdp, ptp), device_id_type=MESH)

    for k in range(1, 8):
        wcopy(k).start()
    wlocal = pltpu.make_async_copy(wrow, w_ref.at[:, lanes], lsem.at[1])
    wlocal.start()
    for d in range(NDEV):
        @pl.when(own != d)
        def _():
            remote(d).start()

        @pl.when(own == d)
        def _():
            local(d).start()
    for k in range(1, 8):
        wcopy(k).wait()
    wlocal.wait()
    for d in range(NDEV):
        h = HALF[d]

        @pl.when(own == d)
        def _():
            local(d).wait()
            for s in range(NDEV):
                @pl.when(me != s)
                def _():
                    pltpu.make_async_remote_copy(
                        src_ref=acc_ref.at[pl.ds(HBASE[d], h), :],
                        dst_ref=got_ref.at[pl.ds((s % 2) * h, h), pl.ds((s // 2) * cols, cols)],
                        send_sem=send.at[d], recv_sem=recv.at[s],
                        device_id=(s // 4, s % 4), device_id_type=MESH).wait_recv()

        @pl.when(own != d)
        def _():
            remote(d).wait_send()


def send_to_owners(acc):
    cols = acc.shape[1]
    return pl.pallas_call(
        owners_kernel,
        out_shape=(jax.ShapeDtypeStruct((CAPMAX, cols * 8), jnp.float32),
                   jax.ShapeDtypeStruct((8, cols * 8), jnp.float32)),
        in_specs=[pl.BlockSpec(memory_space=pltpu.VMEM)],
        out_specs=(pl.BlockSpec(memory_space=pl.ANY), pl.BlockSpec(memory_space=pl.ANY)),
        scratch_shapes=[
            pltpu.SemaphoreType.DMA((NDEV,)),
            pltpu.SemaphoreType.DMA((NDEV,)),
            pltpu.SemaphoreType.DMA((8,)),
            pltpu.SemaphoreType.DMA((8,)),
            pltpu.SemaphoreType.DMA((2,)),
        ],
        compiler_params=pltpu.CompilerParams(collective_id=2, has_side_effects=True),
        name="send_to_owners",
    )(acc)


def expand_kernel(scale, bounds_ref, ids_ref, got_ref, out_ref):
    t = pl.program_id(0)
    half = bounds_ref[OWN_ROWS // TILE + 1]
    base = bounds_ref[OWN_ROWS // TILE + 2] + t * TILE
    out_ref[...] = jnp.zeros_like(out_ref)

    lo, hi = bounds_ref[t], bounds_ref[t + 1]

    def copy(slots):
        rows = [got_ref[pl.ds((s & 1) * half + (s >> 1), 1), :] * scale for s in slots]
        for s, row in zip(slots, rows):
            out_ref[pl.ds(ids_ref[s] - base, 1), :] = row

    def body(i, carry):
        copy([lo + i * 2, lo + i * 2 + 1])
        return carry

    pairs = (hi - lo) // 2
    lax.fori_loop(0, pairs, body, 0)

    @pl.when((hi - lo) % 2 == 1)
    def _():
        copy([hi - 1])


def expand(bounds, ids, got, scale):
    width = got.shape[1]
    return pl.pallas_call(
        functools.partial(expand_kernel, scale),
        grid_spec=pltpu.PrefetchScalarGridSpec(
            num_scalar_prefetch=2, grid=(OWN_ROWS // TILE,),
            in_specs=[pl.BlockSpec((CAPMAX, width), lambda i, *_: (0, 0))],
            out_specs=pl.BlockSpec((TILE, width), lambda i, *_: (i, 0)),
        ),
        out_shape=jax.ShapeDtypeStruct((OWN_ROWS, width), jnp.float32),
        compiler_params=pltpu.CompilerParams(vmem_limit_bytes=60 * 2**20),
        name="expand",
    )(bounds, ids, got)


def norm_kernel(c_ref, slots_ref, near_ref, mine0, mine1, theirs0, theirs1, dyn_ref, dyr_ref, w_ref,
                x_ref, y_ref, g_ref, far, picked, wacc, sems):
    t = pl.program_id(0)
    last = pl.num_programs(0) - 1
    half = FAR_CAP // 2
    width = w_ref.shape[1]

    @pl.when(t == 0)
    def _():
        wacc[...] = jnp.zeros_like(wacc)
        copies = []
        for j, (ref, core) in enumerate(((mine0, c_ref[0]), (mine1, c_ref[0]), (theirs0, 1 - c_ref[0]), (theirs1, 1 - c_ref[0]))):
            at = pl.multiple_of(core * half + (j % 2) * (half // 2), 8)
            copies.append(pltpu.make_async_copy(ref, far.at[pl.ds(at, half // 2), :], sems.at[j]))
        for cp in copies:
            cp.start()
        far[pl.ds(FAR_CAP, 8), :] = jnp.zeros((8, width), jnp.float32)
        for cp in copies:
            cp.wait()

    @pl.when(t < last)
    def _():
        def pick(i, carry):
            rows = [far[pl.ds(slots_ref[t * ROW_TILE + i * 4 + u], 1), :] for u in range(4)]
            for u in range(4):
                picked[pl.ds(i * 4 + u, 1), :] = rows[u]
            return carry

        lax.fori_loop(0, ROW_TILE // 4, pick, 0)
        gain = 1.0 + w_ref[...]

        def body(i, carry):
            at = pl.ds(pl.multiple_of(i * 16, 16), 16)
            xb = (near_ref[at, :] + picked[at, :]).astype(jnp.bfloat16)
            x_ref[at, :] = xb
            xf = xb.astype(jnp.float32)
            r = lax.rsqrt(jnp.sum(xf * xf, axis=1, keepdims=True) * (1.0 / width) + NORM_EPS)
            xh = xf * r
            y_ref[at, :] = (xh * gain).astype(jnp.bfloat16)
            dy = dyn_ref[at, :].astype(jnp.float32)
            wacc[...] += dy * xh
            a = dy * gain
            m = jnp.sum(a * xh, axis=1, keepdims=True) * (1.0 / width)
            g_ref[at, :] = dyr_ref[at, :].astype(jnp.float32) + r * (a - xh * m)
            return carry

        lax.fori_loop(0, ROW_TILE // 16, body, 0)

    @pl.when(t == last)
    def _():
        total = jnp.sum(wacc[...], axis=0, keepdims=True)
        first = lax.broadcasted_iota(jnp.int32, (8, width), 0) == 0
        g_ref[pl.ds(0, 8), :] = jnp.where(first, total, 0.0)


def norm(core, slots, near, far, dyn, dyr, w):
    rows, width = near.shape
    tiles = rows // ROW_TILE
    row = pl.BlockSpec((ROW_TILE, width), lambda i, *_: (jnp.minimum(i, tiles - 1), 0))
    anyspec = pl.BlockSpec(memory_space=pl.ANY)
    return pl.pallas_call(
        norm_kernel,
        grid_spec=pltpu.PrefetchScalarGridSpec(
            num_scalar_prefetch=2, grid=(tiles + 1,),
            in_specs=[row] + [anyspec] * 4 + [row, row, pl.BlockSpec((1, width), lambda i, *_: (0, 0))],
            out_specs=[row, row, pl.BlockSpec((ROW_TILE, width), lambda i, *_: (i, 0))],
            scratch_shapes=[
                pltpu.VMEM((FAR_CAP + 8, width), jnp.float32),
                pltpu.VMEM((ROW_TILE, width), jnp.float32),
                pltpu.VMEM((16, width), jnp.float32),
                pltpu.SemaphoreType.DMA((4,)),
            ],
        ),
        out_shape=(jax.ShapeDtypeStruct((rows, width), jnp.bfloat16),
                   jax.ShapeDtypeStruct((rows, width), jnp.bfloat16),
                   jax.ShapeDtypeStruct((rows + 8, width), jnp.float32)),
        compiler_params=pltpu.CompilerParams(vmem_limit_bytes=60 * 2**20),
        name="assemble_norm",
    )(core, slots, near, *far, dyn, dyr, w)


def solution(mesh):
    def plan(all_ids, rows):
        n = all_ids.shape[0]
        dp, tp = lax.axis_index("dp"), lax.axis_index("tp")
        me, core = tp * 4 + dp, tp % 2
        keys = lax.sort(all_ids * n + lax.iota(jnp.int32, n), is_stable=False)
        ids, idx = keys >> 13, keys & (n - 1)
        differs = ids[1:] != ids[:-1]
        one = jnp.ones((1,), jnp.int32)
        first = jnp.concatenate([one, differs.astype(jnp.int32)])
        slot = jnp.cumsum(first) - 1
        edges = jnp.arange(NDEV + 1, dtype=jnp.int32) * OWN_ROWS
        starts = jnp.sum(jnp.where(ids[None, :] < edges[:, None], first[None, :], 0), axis=1)
        caps = jnp.array(CAPS, jnp.int32)
        overflow = jnp.any(starts[1:] - starts[:-1] > caps)
        chip = idx >> 10
        fresh = jnp.concatenate([one, (differs | (chip[1:] != chip[:-1])).astype(jnp.int32)])
        far = jnp.where((ids >> 15) != (chip & 1), fresh, 0)
        per_chip = jnp.sum(jnp.where(chip[None, :] == jnp.arange(8, dtype=jnp.int32)[:, None], far[None, :], 0), axis=1)
        overflow = overflow | jnp.any(per_chip > FAR_CAP)
        owner = ids // OWN_ROWS
        hit = owner[None, :] == jnp.arange(NDEV, dtype=jnp.int32)[:, None]
        offset = jnp.sum(jnp.where(hit, starts[:-1][:, None], 0), axis=0)
        hbase = jnp.sum(jnp.where(hit, jnp.array(HBASE, jnp.int32)[:, None], 0), axis=0)
        local_slot = slot - offset
        pos = jnp.minimum(hbase + local_slot // 2, HTOT - 1)
        mine = local_slot % 2 == core
        src = (idx // 512) * rows + idx % 512
        work = lax.sort(jnp.where(mine, 0, 1 << 26) + src * 4096 + pos, is_stable=False)
        count = jnp.sum(mine.astype(jnp.int32)).reshape(1)
        uniq = lax.sort(jnp.where(first == 1, ids, 1 << 20), is_stable=False)
        uniq = jnp.concatenate([uniq, jnp.full((CAPMAX,), 1 << 20, jnp.int32)])
        my_start = jnp.sum(jnp.where(jnp.arange(NDEV) == me, starts[:-1], 0))
        my_ids = lax.dynamic_slice(uniq, (my_start,), (CAPMAX,))
        tiles = me * OWN_ROWS + jnp.arange(OWN_ROWS // TILE + 1, dtype=jnp.int32) * TILE
        bounds = jnp.sum(jnp.where(ids[None, :] < tiles[:, None], first[None, :], 0), axis=1) - my_start
        my_half = jnp.sum(jnp.where(jnp.arange(NDEV) == me, jnp.array(HALF, jnp.int32), 0))
        bounds = jnp.concatenate([bounds, my_half[None], (me * OWN_ROWS)[None]]).astype(jnp.int32)
        return overflow, work, count, my_ids, bounds

    def far_lists(ids):
        n = ids.shape[1]
        pos = lax.iota(jnp.int32, n)
        same = ids[:, :, None] == ids[:, None, :]
        lead = jnp.min(jnp.where(same, pos[None, :, None], n), axis=1)
        far = (ids >> 15) != jnp.arange(2, dtype=jnp.int32)[:, None]
        first = (lead == pos[None]) & far
        slot = jnp.sum(jnp.where(first[:, :, None] & (pos[None, :, None] < lead[:, None, :]), 1, 0), axis=1)
        slots = lax.iota(jnp.int32, FAR_CAP)
        at = first[:, :, None] & (slot[:, :, None] == slots[None, None, :])
        listed = jnp.max(jnp.where(at, ids[:, :, None], -1), axis=1)
        return listed, jnp.where(far, jnp.minimum(slot, FAR_CAP - 1), FAR_CAP)

    def local_step(tokens, emb_table, w_norm, dy_norm, dy_resid):
        shard_rows, model_dim = emb_table.shape
        scale_float = jnp.asarray(math.sqrt(model_dim), jnp.bfloat16).astype(jnp.float32)
        scale_py = float(np.array(math.sqrt(model_dim)).astype(jnp.dtype(jnp.bfloat16)))
        dp, tp = lax.axis_index("dp"), lax.axis_index("tp")
        x, c = tp // 2, tp % 2
        seq = tokens.shape[1]
        part = seq // 4
        swap_core = [(t, t ^ 1) for t in range(4)]
        swap_x = [(t, t ^ 2) for t in range(4)]

        def fetch(ids):
            ids = ids - tp * shard_rows
            owned = (ids >= 0) & (ids < shard_rows)
            got = jnp.take(emb_table, jnp.where(owned, ids, 0), axis=0, mode="clip")
            return jnp.where(owned[:, None], got.astype(jnp.float32) * scale_float, 0.0)

        def positions(toks, px, pc):
            return lax.dynamic_slice(toks, ((px * 2 + pc) * part,), (part,))

        listed, slots = far_lists(tokens.reshape(2, seq // 2))
        my_list = jnp.where(x == 0, listed[1], listed[0])
        my_slots = lax.dynamic_slice(slots.reshape(-1), (tp * part,), (part,))
        half, n = FAR_CAP // 2, FAR_CAP // 2 // FWD_CHUNKS
        got, toks = [], tokens[0]
        for k in range(FWD_CHUNKS):
            theirs = lax.dynamic_slice(my_list, ((1 - c) * half + k * n,), (n,))
            mine = lax.dynamic_slice(my_list, (c * half + k * n,), (n,))
            both = fetch(theirs)
            both = lax.ppermute(both, "tp", swap_core)
            both = both + fetch(mine)
            both, my_list, toks = lax.optimization_barrier((both, my_list, toks))
            got.append(lax.ppermute(both, "tp", swap_x))
        relayed = [lax.ppermute(r, "tp", swap_core) for r in got]
        all_ids = lax.all_gather(toks[None], "dp", axis=0, tiled=True).reshape(-1)
        near = fetch(positions(toks, x, 1 - c))
        near = lax.ppermute(near, "tp", swap_core)
        near = near + fetch(positions(toks, x, c))
        rows = part + 8
        overflow, work, count, my_ids, bounds = plan(all_ids, rows)

        def dense_forward(near, toks):
            far = lax.ppermute(fetch(positions(toks, 1 - x, 1 - c)), "tp", swap_core) + fetch(positions(toks, 1 - x, c))
            x_emb = (near + lax.ppermute(far, "tp", swap_x)).astype(jnp.bfloat16)
            x_float = x_emb.astype(jnp.float32)
            inv_rms = lax.rsqrt(jnp.mean(x_float * x_float, axis=-1, keepdims=True) + NORM_EPS)
            x_hat = x_float * inv_rms
            norm_gain = 1.0 + w_norm
            y_norm = (x_hat * norm_gain).astype(jnp.bfloat16)
            dy_float = dy_norm[0].astype(jnp.float32)
            dx_hat = dy_float * norm_gain
            tok_grad = dy_resid[0].astype(jnp.float32) + inv_rms * (dx_hat - x_hat * jnp.mean(dx_hat * x_hat, axis=-1, keepdims=True))
            w_part = jnp.sum(dy_float * x_hat, axis=0)
            return x_emb, y_norm, jnp.concatenate([tok_grad, jnp.pad(w_part[None], ((0, 7), (0, 0)))], axis=0)

        def sparse_forward(near, toks):
            core = c.astype(jnp.int32).reshape(1)
            return tuple(norm(core, my_slots, near, got + relayed, dy_norm[0], dy_resid[0], w_norm[None]))

        x_emb, y_norm, g_ext = lax.cond(overflow, dense_forward, sparse_forward, near, toks)

        cols = exchange_columns(g_ext)
        acc = sum_duplicates(work, count, cols, part)
        owned, w_rows = send_to_owners(acc)

        def dense_backward(g_ext, owned):
            g = g_ext[:part]
            ids = tokens[0] - tp * shard_rows
            seq_grad = jnp.zeros((seq, model_dim), jnp.float32)
            for s in range(4):
                block = g if s == 0 else lax.ppermute(g, "tp", [(t, (t + s) % 4) for t in range(4)])
                seq_grad = lax.dynamic_update_slice(seq_grad, block, ((tp + 4 - s) % 4 * part, 0))
            drop_ids = jnp.where((ids >= 0) & (ids < shard_rows), ids, shard_rows)
            shard_grad = jax.ops.segment_sum(seq_grad, drop_ids, num_segments=shard_rows, mode="drop") * scale_float
            total = lax.dynamic_slice(shard_grad, (dp * OWN_ROWS, 0), (OWN_ROWS, model_dim))
            for s in range(1, 4):
                block = lax.dynamic_slice(shard_grad, ((dp + s) % 4 * OWN_ROWS, 0), (OWN_ROWS, model_dim))
                total = total + lax.ppermute(block, "dp", [(d, (d + s) % 4) for d in range(4)])
            return total

        def sparse_backward(g_ext, owned):
            return expand(bounds, my_ids, owned, scale_py)

        emb_grad = lax.cond(overflow, dense_backward, sparse_backward, g_ext, owned)
        return x_emb[None], y_norm[None], emb_grad, w_rows[0]

    act_spec = P("dp", "tp", None)
    return jax.shard_map(local_step, mesh=mesh, in_specs=(P("dp", None), P("tp", None), P(None), act_spec, act_spec), out_specs=(act_spec, act_spec, P(("tp", "dp"), None), P(None)), check_vma=False)
```

profile of v0, /device:TPU:0, one launch (start us, length us, event | category | flops | bytes accessed | tf_op | source)
XLA Modules:
  0.0 550.5 jit_solution(5633077857680672391)
XLA Ops:
  1.2 1.4 reduce.10
  2.6 1.3 select_reduce_fusion.1
  3.9 1.8 select_reduce_fusion
  5.7 1.6 select_reduce_fusion.2
  7.4 10.4 %gather_fusion.2 = bf16[160,3072]{1,0:T(8,128)(2,1)S(1)} fusion(bf16[16384,3072]{1,0:T(8,128)(2,1)} %param.13, s32[1024]{0:T(1024)S(1)} %pad_clamp_fusion.7), kind=kCustom, calls=%fused_computation.2 | custom fusion | bytes 1966720 | tf_op jit(solution)/shard_map/jit(_take)/gather | solution.py:446
  19.3 10.3 %gather_fusion.3 = bf16[160,3072]{1,0:T(8,128)(2,1)S(1)} fusion(bf16[16384,3072]{1,0:T(8,128)(2,1)} %param.13, s32[1024]{0:T(1024)S(1)} %pad_clamp_fusion.6), kind=kCustom, calls=%fused_computation.3 | custom fusion | bytes 1966720 | tf_op jit(solution)/shard_map/jit(_take)/gather | solution.py:446
  29.6 3.2 select_add_fusion.3
  32.9 10.2 %gather_fusion.4 = bf16[160,3072]{1,0:T(8,128)(2,1)S(1)} fusion(bf16[16384,3072]{1,0:T(8,128)(2,1)} %param.13, s32[1024]{0:T(1024)S(1)} %pad_clamp_fusion.5), kind=kCustom, calls=%fused_computation.4 | custom fusion | bytes 1966720 | tf_op jit(solution)/shard_map/jit(_take)/gather | solution.py:446
  43.1 1.6 multiply_select_fusion.2
  44.7 1.4 collective-permute-start.9
  46.2 10.3 %gather_fusion.5 = bf16[160,3072]{1,0:T(8,128)(2,1)S(1)} fusion(bf16[16384,3072]{1,0:T(8,128)(2,1)} %param.13, s32[1024]{0:T(1024)S(1)} %pad_clamp_fusion.4), kind=kCustom, calls=%fused_computation.5 | custom fusion | bytes 1966720 | tf_op jit(solution)/shard_map/jit(_take)/gather | solution.py:446
  56.5 1.6 select_add_fusion.2
  58.2 12.3 %gather_fusion.6 = bf16[512,3072]{1,0:T(8,128)(2,1)S(1)} fusion(bf16[16384,3072]{1,0:T(8,128)(2,1)} %param.13, s32[1024]{0:T(1024)S(1)} %pad_clamp_fusion.3), kind=kCustom, calls=%fused_computation.6 | custom fusion | bytes 6293504 | tf_op jit(solution)/shard_map/jit(_take)/gather | solution.py:446
  70.6 3.7 multiply_select_fusion.1
  74.3 9.8 %collective-permute-start.10 = (f32[512,3072]{1,0:T(8,128)}, f32[512,3072]{1,0:T(8,128)}, u32[]{:S(2)}, u32[]{:S(2)}) collective-permute-start(f32[512,3072]{1,0:T(8,128)} %multiply_select_fusion.1), channel_id=1, source_target_pairs={{0,1},{1,0},{2,3},{3,2},{4,5},{5,4},{6,7},{7,6},{8,9},{9,8},{10,11... | collective-permute-start | bytes 18874376 | tf_op jit(solution)/shard_map/ppermute | solution.py:468
  84.0 6.8 %collective-permute-start.11 = (f32[160,3072]{1,0:T(8,128)}, f32[160,3072]{1,0:T(8,128)}, u32[]{:S(2)}, u32[]{:S(2)}) collective-permute-start(f32[160,3072]{1,0:T(8,128)} %select_add_fusion.3), channel_id=1, source_target_pairs={{0,2},{1,3},{2,0},{3,1},{4,6},{5,7},{6,4},{7,5},{8,10},{9,11},{10,... | collective-permute-start | bytes 5898248 | tf_op jit(solution)/shard_map/ppermute | solution.py:464
  90.9 8.6 %all-gather = s32[8192]{0:T(1024)S(1)} all-gather(s32[2048]{0:T(1024)S(1)} %bitcast.47), channel_id=2, replica_groups=mesh['dp'=4,'tp'=4] {'dp'}, dimensions={0}, use_global_device_ids=true | all-gather | bytes 40960 | tf_op jit(solution)/shard_map/all_gather | solution.py:466
  99.4 5.6 %sort.21 = s32[8192]{0:T(1024)S(1)} sort(s32[8192]{0:T(1024)S(1)} %multiply_add_fusion), dimensions={0}, to_apply=%region_3.4 | sort | flops 106496 | bytes 65536 | tf_op jit(solution)/shard_map/sort | solution.py:384
  105.7 29.1 %collective-permute-done.11 = f32[160,3072]{1,0:T(8,128)} collective-permute-done((f32[160,3072]{1,0:T(8,128)}, f32[160,3072]{1,0:T(8,128)}, u32[]{:S(2)}, u32[]{:S(2)}) %collective-permute-start.11) | collective-permute-done | bytes 1966112 | tf_op jit(solution)/shard_map/ppermute | solution.py:464
  137.1 39.4 %collective-permute-done.12 = f32[160,3072]{1,0:T(8,128)} collective-permute-done((f32[160,3072]{1,0:T(8,128)}, f32[160,3072]{1,0:T(8,128)}, u32[]{:S(2)}, u32[]{:S(2)}) %collective-permute-start.12) | collective-permute-done | bytes 1966112 | tf_op jit(solution)/shard_map/ppermute | solution.py:464
  179.3 6.2 %sort.23.work_ref = s32[8192]{0:T(1024)} sort(s32[8192]{0:T(1024)S(1)} %get-tuple-element.194), dimensions={0}, to_apply=%region_21.22 | sort | flops 106496 | bytes 65536 | tf_op jit(solution)/shard_map/sort | solution.py:407
  185.5 5.6 %sort.22 = s32[8192]{0:T(1024)S(1)} sort(s32[8192]{0:T(1024)S(1)} %get-tuple-element.195), dimensions={0}, to_apply=%region_16.17 | sort | flops 106496 | bytes 65536 | tf_op jit(solution)/shard_map/sort | solution.py:409
  191.2 28.3 %gather_fusion.7 = bf16[512,3072]{1,0:T(8,128)(2,1)} fusion(bf16[16384,3072]{1,0:T(8,128)(2,1)} %param.13, s32[1024]{0:T(1024)S(1)} %pad_clamp_fusion.2), kind=kCustom, calls=%fused_computation.7 | custom fusion | bytes 6293504 | tf_op jit(solution)/shard_map/jit(_take)/gather | solution.py:446
  221.2 8.1 %select_add_fusion.1 = f32[512,3072]{1,0:T(8,128)} fusion(f32[512,3072]{1,0:T(8,128)} %collective-permute-done.10, bf16[512,3072]{1,0:T(8,128)(2,1)} %gather_fusion.7, pred[512]{0:T(512)(128)(4,1)S(1)} %get-tuple-element.173), kind=kLoop, calls=%fused_computation.60 | loop fusion | flops 6291456 | bytes 15729152 | tf_op jit(solution)/shard_map/add | solution.py:469
  229.3 20.6 %conditional.2 = (f32[520,3072]{1,0:T(8,128)}, bf16[512,3072]{1,0:T(8,128)(2,1)}, bf16[512,3072]{1,0:T(8,128)(2,1)}) conditional(s32[]{:T(128)} %convert_element_type.64, (s32[]{:T(128)}, s32[2048]{0:T(1024)S(1)}, s32[2,1024]{1,0:T(2,128)S(1)}, s32[2,1024]{1,0:T(2,128)S(1)}, s32[]{:T(128)}, /*index=5*/bf16[1,512,3072]{2,1,0:T(8,128)(2,1)S(1)}, ...), branch_computations={%region_8.9_spmd, %region_9.13_spmd} | conditional | flops 53558800 | bytes 166941024 | solution.py:491
  230.0 19.9 %assemble_norm.1 = (bf16[512,3072]{1,0:T(8,128)(2,1)}, bf16[512,3072]{1,0:T(8,128)(2,1)}, f32[520,3072]{1,0:T(8,128)}) custom-call(s32[1]{0:T(128)} %bitcast.c_ref, s32[512]{0:T(512)} %dynamic-slice_select_fusion.slots_ref, f32[512,3072]{1,0:T(8,128)} %get-tuple-element.108.near_ref, f32[160,3072]{1,0:T(8,128)} %get-tuple-element.109.mine0, ...), custom_call_target="tpu_custom_call" | custom-call | tf_op jit(solution)/shard_map/cond/branch_0_fun/assemble_norm/pallas_call | solution.py:358
  249.9 107.7 %exchange_columns.1 = f32[16,520,384]{2,1,0:T(8,128)} custom-call(f32[520,3072]{1,0:T(8,128)} %get-tuple-element.157.g_ref), custom_call_target="tpu_custom_call" | custom-call | tf_op jit(solution)/shard_map/exchange_columns/pallas_call | solution.py:93
  357.6 28.5 %sum_duplicates.1.acc_ref = f32[2904,384]{1,0:T(8,128)} custom-call(s32[8192]{0:T(1024)} %sort.23.work_ref, s32[1]{0:T(128)} %bitcast.20.count_ref, f32[8320,384]{1,0:T(8,128)} %bitcast.42), custom_call_target="tpu_custom_call" | custom-call | tf_op jit(solution)/shard_map/sum_duplicates/pallas_call | solution.py:151
  386.1 124.0 %send_to_owners.1 = (f32[1536,3072]{1,0:T(8,128)}, f32[8,3072]{1,0:T(8,128)}) custom-call(f32[2904,384]{1,0:T(8,128)} %sum_duplicates.1.acc_ref), custom_call_target="tpu_custom_call" | custom-call | tf_op jit(solution)/shard_map/send_to_owners/pallas_call | solution.py:240
  510.2 1.5 slice.49
  511.7 37.5 %conditional.3 = (f32[4096,3072]{1,0:T(8,128)}) conditional(s32[]{:T(128)} %convert_element_type.64, (s32[8192]{0:T(1024)S(1)}, s32[]{:T(128)}, s32[35]{0:T(128)S(1)}, f32[1536,3072]{1,0:T(8,128)}) %tuple.38, (s32[]{:T(128)}, s32[1,2048]{1,0:T(1,128)S(1)}, f32[520,3072]{1,0:T(8,128)}, s32[]{:T(128)}) %tuple.80), branch_computations={%region_23.24_spmd, %region_24.26_spmd} | conditional | flops 94382144 | bytes 2019975552 | solution.py:515
  514.4 34.6 %expand.1 = f32[4096,3072]{1,0:T(8,128)} custom-call(s32[35]{0:T(128)S(1)} %get-tuple-element.128.bounds_ref, s32[1536]{0:T(1024)} %pad_dynamic-slice_fusion.ids_ref, f32[1536,3072]{1,0:T(8,128)} %get-tuple-element.131.got_ref), custom_call_target="tpu_custom_call" | custom-call | tf_op jit(solution)/shard_map/cond/branch_0_fun/expand/pallas_call | solution.py:285
  (65 shorter events, 10.0 us)
Async XLA Ops:
  18.1 11.6 %collective-permute-start.8 = (f32[160,3072]{1,0:T(8,128)S(1)}, f32[160,3072]{1,0:T(8,128)}, u32[]{:S(2)}, u32[]{:S(2)}) collective-permute-start(f32[160,3072]{1,0:T(8,128)S(1)} %multiply_select_fusion.3), channel_id=1, source_target_pairs={{0,1},{1,0},{2,3},{3,2},{4,5},{5,4},{6,7},{7,6},{8,9},{9,8},{10,11... | collective-permute-start | bytes 5898248 | tf_op jit(solution)/shard_map/ppermute | solution.py:461
  44.7 11.8 %collective-permute-start.9 = (f32[160,3072]{1,0:T(8,128)}, f32[160,3072]{1,0:T(8,128)S(1)}, u32[]{:S(2)}, u32[]{:S(2)}) collective-permute-start(f32[160,3072]{1,0:T(8,128)} %multiply_select_fusion.2), channel_id=1, source_target_pairs={{0,1},{1,0},{2,3},{3,2},{4,5},{5,4},{6,7},{7,6},{8,9},{9,8},{10,11... | collective-permute-start | bytes 5898248 | tf_op jit(solution)/shard_map/ppermute | solution.py:461
  46.2 12.0 %copy-start.4 = (s32[1,2048]{1,0:T(1,128)S(1)}, s32[1,2048]{1,0:T(1,128)}, u32[]{:S(2)}) copy-start(s32[1,2048]{1,0:T(1,128)} %param.12) | copy-start | bytes 24580
  70.5 64.7 %copy-start.8 = (s32[16]{0:T(128)S(1)}, s32[16]{0:T(128)}, u32[]{:S(2)}) copy-start(s32[16]{0:T(128)} %constant.264.clone) | copy-start | bytes 196
  70.6 65.4 %copy-start.6 = (s32[16]{0:T(128)S(1)}, s32[16]{0:T(128)}, u32[]{:S(2)}) copy-start(s32[16]{0:T(128)} %constant.263.clone) | copy-start | bytes 196
  70.6 106.8 %copy-start.7 = (s32[16]{0:T(128)S(1)}, s32[16]{0:T(128)}, u32[]{:S(2)}) copy-start(s32[16]{0:T(128)} %constant.262.clone) | copy-start | bytes 196
  74.3 146.9 %collective-permute-start.10 = (f32[512,3072]{1,0:T(8,128)}, f32[512,3072]{1,0:T(8,128)}, u32[]{:S(2)}, u32[]{:S(2)}) collective-permute-start(f32[512,3072]{1,0:T(8,128)} %multiply_select_fusion.1), channel_id=1, source_target_pairs={{0,1},{1,0},{2,3},{3,2},{4,5},{5,4},{6,7},{7,6},{8,9},{9,8},{10,11... | collective-permute-start | bytes 18874376 | tf_op jit(solution)/shard_map/ppermute | solution.py:468
  84.0 50.8 %collective-permute-start.11 = (f32[160,3072]{1,0:T(8,128)}, f32[160,3072]{1,0:T(8,128)}, u32[]{:S(2)}, u32[]{:S(2)}) collective-permute-start(f32[160,3072]{1,0:T(8,128)} %select_add_fusion.3), channel_id=1, source_target_pairs={{0,2},{1,3},{2,0},{3,1},{4,6},{5,7},{6,4},{7,5},{8,10},{9,11},{10,... | collective-permute-start | bytes 5898248 | tf_op jit(solution)/shard_map/ppermute | solution.py:464
  90.8 85.7 %collective-permute-start.12 = (f32[160,3072]{1,0:T(8,128)}, f32[160,3072]{1,0:T(8,128)}, u32[]{:S(2)}, u32[]{:S(2)}) collective-permute-start(f32[160,3072]{1,0:T(8,128)} %select_add_fusion.2), channel_id=1, source_target_pairs={{0,2},{1,3},{2,0},{3,1},{4,6},{5,7},{6,4},{7,5},{8,10},{9,11},{10,... | collective-permute-start | bytes 5898248 | tf_op jit(solution)/shard_map/ppermute | solution.py:464
  134.8 94.4 %collective-permute-start.13 = (f32[160,3072]{1,0:T(8,128)}, f32[160,3072]{1,0:T(8,128)}, u32[]{:S(2)}, u32[]{:S(2)}) collective-permute-start(f32[160,3072]{1,0:T(8,128)} %collective-permute-done.11), channel_id=1, source_target_pairs={{0,1},{1,0},{2,3},{3,2},{4,5},{5,4},{6,7},{7,6},{8,9},{9,8},{10,11... | collective-permute-start | bytes 5898248 | tf_op jit(solution)/shard_map/ppermute | solution.py:465
  176.5 52.7 %collective-permute-start.14 = (f32[160,3072]{1,0:T(8,128)}, f32[160,3072]{1,0:T(8,128)}, u32[]{:S(2)}, u32[]{:S(2)}) collective-permute-start(f32[160,3072]{1,0:T(8,128)} %collective-permute-done.12), channel_id=1, source_target_pairs={{0,1},{1,0},{2,3},{3,2},{4,5},{5,4},{6,7},{7,6},{8,9},{9,8},{10,11... | collective-permute-start | bytes 5898248 | tf_op jit(solution)/shard_map/ppermute | solution.py:465
  221.2 8.1 %copy-start = (bf16[1,512,3072]{2,1,0:T(8,128)(2,1)S(1)}, bf16[1,512,3072]{2,1,0:T(8,128)(2,1)}, u32[]{:S(2)}) copy-start(bf16[1,512,3072]{2,1,0:T(8,128)(2,1)} %param.15) | copy-start | bytes 9437188
  221.2 8.1 %copy-start.5 = (f32[3072]{0:T(1024)S(1)}, f32[3072]{0:T(1024)}, u32[]{:S(2)}) copy-start(f32[3072]{0:T(1024)} %param.14) | copy-start | bytes 36868
where the time goes:
time: 561 us; the launch traced here: 550 us
  Pallas kernels  315 us (56%)
  local copies, waits for them, and re-layouts  84.8 us (15%)
  waiting for transfers between devices  68.5 us (12%)
  other arithmetic  48.8 us (9%)
  starting transfers between devices  19.2 us (3%)
  blocking collectives  8.57 us (2%)
    pallas_call x1, Pallas kernels, send_to_owners(): pl.pallas_call(owners_kernel, out_shape=(jax.ShapeDtypeStruct((CAPMAX, co...  124 us
    pallas_call x1, Pallas kernels, exchange_columns(): pl.pallas_call(columns_kernel, out_shape=jax.ShapeDtypeStruct((NDEV, rows...  108 us
    gather x6, local copies, waits for them, and re-layouts, fetch(): got = jnp.take(emb_table, jnp.where(owned, ids, 0), axis=0, mode='clip')  81.9 us
    ppermute x2, waiting for transfers between devices, local_step(): got.append(lax.ppermute(both, 'tp', swap_x))  68.5 us
    pallas_call x1, Pallas kernels, expand(): pl.pallas_call(functools.partial(expand_kernel, scale), grid_spec=pltpu.P...  34.6 us
    pallas_call x1, Pallas kernels, sum_duplicates(): pl.pallas_call(functools.partial(sum_kernel, rows, tok_rows), grid_spec=p...  28.5 us
    pallas_call x1, Pallas kernels, norm(): pl.pallas_call(norm_kernel, grid_spec=pltpu.PrefetchScalarGridSpec(num_sc...  19.9 us
  transfers between devices with their start and end apart: 7, of which 2 were waited for; matrix products, arithmetic and copies ran while one was open for 15% of the time, Pallas kernels for 0%

commit v1 on v0

--- a/solution.py
+++ b/solution.py
@@ -12,13 +12,14 @@
 MESH = pl.DeviceIdType.MESH
 NDEV = 16
 OWN_ROWS = 4096
-CAPS = (1536, 576, 368, 368) + (288,) * 4 + (224,) * 8
+CAPS = (1536, 544, 352, 352) + (256,) * 4 + (208,) * 8
 HALF = tuple(c // 2 for c in CAPS)
 HBASE = tuple(sum(HALF[:i]) for i in range(NDEV))
 HTOT = sum(HALF)
 CAPMAX = max(CAPS)
 FAR_CAP = 640
-FWD_CHUNKS = 2
+FAR_CHUNKS = (128, 192)
+NEAR_PIECE = 256
 ROW_TILE = 64
 ACCS = 4
 UNROLL = 4
@@ -30,59 +31,112 @@
     return dp // 2, dp % 2, tp // 2, tp % 2
 
 
-def peer(z, y, x, c, k):
-    pz, py, px = (z + k // 4) % 2, (y + (k // 2) % 2) % 2, (x + k % 2) % 2
-    dp, tp = pz * 2 + py, px * 2 + c
-    return dp, tp, dp * 2 + px
-
-
-def columns_kernel(g_ref, out_ref, stage, send, recv, fsend, frecv, lsem):
-    z, y, x, c = coords()
-    dp = z * 2 + y
-    q = dp * 2 + x
+def flip(pos, dims):
+    z, y, x, c = pos
+    return ((1 - z if 2 in dims else z), (1 - y if 1 in dims else y), (1 - x if 0 in dims else x), c)
+
+
+def chip_of(pos):
+    z, y, x, _ = pos
+    return z * 4 + y * 2 + x
+
+
+def device_of(pos):
+    z, y, x, c = pos
+    return z * 2 + y, x * 2 + c
+
+
+def bits(k):
+    return tuple(d for d in range(3) if k >> d & 1)
+
+
+def hops(third, k):
+    return tuple(d for d in ((third + i) % 3 for i in range(3)) if k >> d & 1)
+
+
+def kinds(third):
+    a, b, c = (1 << ((third + i) % 3) for i in range(3))
+    return (7, a + b, a + c, b + c, a, b, c)
+
+
+HOP_ID = {}
+for _t in range(3):
+    for _k in range(1, 8):
+        for _h in range(len(hops(_t, _k))):
+            HOP_ID[_t, _k, _h] = len(HOP_ID)
+RELAY_ID = {}
+for _t, _k, _h in HOP_ID:
+    if _h + 1 < len(hops(_t, _k)):
+        RELAY_ID[_t, _k, _h] = len(RELAY_ID)
+
+
+def columns_kernel(g_ref, out_ref, stage, relay, send, recv, fsend, frecv, lsem):
+    me = coords()
+    q, c = chip_of(me), me[3]
     cols = out_ref.shape[2]
-    partner = (dp, x * 2 + (1 - c))
+    third = cols // 3
+    partner = device_of(me[:3] + (1 - c,))
     barrier = pltpu.get_barrier_semaphore()
-    for k in range(1, 8):
-        pdp, ptp, _ = peer(z, y, x, c, k)
-        pl.semaphore_signal(barrier, inc=1, device_id=(pdp, ptp), device_id_type=MESH)
+    for d in range(3):
+        pl.semaphore_signal(barrier, inc=1, device_id=device_of(flip(me, (d,))), device_id_type=MESH)
     pl.semaphore_signal(barrier, inc=1, device_id=partner, device_id_type=MESH)
-    pl.semaphore_wait(barrier, 8)
-
-    def block(qq):
-        return g_ref.at[:, pl.ds(pl.multiple_of(qq * cols, 128), cols)]
-
-    sends = []
-    for k in (7, 3, 5, 6, 1, 2, 4):
-        pdp, ptp, pq = peer(z, y, x, c, k)
-        cp = pltpu.make_async_remote_copy(
-            src_ref=block(pq), dst_ref=out_ref.at[q * 2 + c],
-            send_sem=send.at[k], recv_sem=recv.at[k],
-            device_id=(pdp, ptp), device_id_type=MESH)
-        cp.start()
-        sends.append((k, pq, cp))
-    fwd = pltpu.make_async_remote_copy(
-        src_ref=block(q), dst_ref=out_ref.at[q * 2 + c],
+    pl.semaphore_wait(barrier, 4)
+
+    def block(chip, at, width):
+        return g_ref.at[:, pl.ds(pl.multiple_of(chip * cols + at, 128), width)]
+
+    def landed(src, t):
+        return out_ref.at[chip_of(src) * 2 + c, :, pl.ds(t * third, third)]
+
+    def hop(t, k, h):
+        dims = hops(t, k)
+        if h == 0:
+            src = block(chip_of(flip(me, dims)), t * third, third)
+        else:
+            src = relay.at[RELAY_ID[t, k, h - 1]]
+        if h + 1 < len(dims):
+            dst = relay.at[RELAY_ID[t, k, h]]
+        else:
+            dst = landed(flip(me, dims[:h]), t)
+        n = HOP_ID[t, k, h]
+        return pltpu.make_async_remote_copy(
+            src_ref=src, dst_ref=dst, send_sem=send.at[n], recv_sem=recv.at[n],
+            device_id=device_of(flip(me, dims[h:h + 1])), device_id_type=MESH)
+
+    for i in range(7):
+        for t in range(3):
+            hop(t, kinds(t)[i], 0).start()
+    own = pltpu.make_async_remote_copy(
+        src_ref=block(q, 0, cols), dst_ref=out_ref.at[q * 2 + c],
         send_sem=fsend.at[0], recv_sem=frecv.at[0],
         device_id=partner, device_id_type=MESH)
-    fwd.start()
-    forwards = [fwd]
-    cin = pltpu.make_async_copy(block(q), stage, lsem.at[0])
+    own.start()
+    cin = pltpu.make_async_copy(block(q, 0, cols), stage, lsem.at[0])
     cin.start()
     cin.wait()
     cout = pltpu.make_async_copy(stage, out_ref.at[q * 2 + c], lsem.at[1])
     cout.start()
-    for k, pq, cp in sorted(sends, key=lambda s: bin(s[0]).count("1")):
-        cp.wait_recv()
-        f = pltpu.make_async_remote_copy(
-            src_ref=out_ref.at[pq * 2 + c], dst_ref=out_ref.at[pq * 2 + c],
-            send_sem=fsend.at[k], recv_sem=frecv.at[k],
-            device_id=partner, device_id_type=MESH)
-        f.start()
-        forwards.append(f)
+    for i, h in ((0, 1), (1, 1), (2, 1), (3, 1), (0, 2)):
+        for t in range(3):
+            k = kinds(t)[i]
+            hop(t, k, h - 1).wait_recv()
+            hop(t, k, h).start()
+    forwards = []
+    for i in (4, 5, 6, 1, 2, 3, 0):
+        for t in range(3):
+            k = kinds(t)[i]
+            hop(t, k, len(hops(t, k)) - 1).wait_recv()
+            here = landed(flip(me, bits(k)), t)
+            f = pltpu.make_async_remote_copy(
+                src_ref=here, dst_ref=here,
+                send_sem=fsend.at[k * 3 + t], recv_sem=frecv.at[k * 3 + t],
+                device_id=partner, device_id_type=MESH)
+            f.start()
+            forwards.append(f)
     cout.wait()
-    for k, pq, cp in sends:
-        cp.wait_send()
+    for t, k, h in HOP_ID:
+        hop(t, k, h).wait_send()
+    own.wait()
     for f in forwards:
         f.wait()
 
@@ -97,10 +151,11 @@
         out_specs=pl.BlockSpec(memory_space=pl.ANY),
         scratch_shapes=[
             pltpu.VMEM((rows, cols), g.dtype),
-            pltpu.SemaphoreType.DMA((8,)),
-            pltpu.SemaphoreType.DMA((8,)),
-            pltpu.SemaphoreType.DMA((8,)),
-            pltpu.SemaphoreType.DMA((8,)),
+            pltpu.VMEM((len(RELAY_ID), rows, cols // 3), g.dtype),
+            pltpu.SemaphoreType.DMA((len(HOP_ID),)),
+            pltpu.SemaphoreType.DMA((len(HOP_ID),)),
+            pltpu.SemaphoreType.DMA((24,)),
+            pltpu.SemaphoreType.DMA((24,)),
             pltpu.SemaphoreType.DMA((2,)),
         ],
         compiler_params=pltpu.CompilerParams(collective_id=1, has_side_effects=True),
@@ -162,13 +217,20 @@
     )(work, count, got.reshape(NDEV * rows, cols))
 
 
-def owners_kernel(acc_ref, got_ref, w_ref, send, recv, wsend, wrecv, lsem):
-    z, y, x, c = coords()
-    dp, tp = z * 2 + y, x * 2 + c
-    q = dp * 2 + x
-    me = q * 2 + c
+RELAYS = {3: 2, 5: 1, 6: 4}
+RELAYED = {r: q for q, r in RELAYS.items()}
+NEIGHBOURS = (1, 2, 4)
+
+
+def owners_kernel(acc_ref, got_ref, w_ref, relay, send, recv, wsend, wrecv, psend, precv, rsend, rrecv, lsem):
+    me = coords()
+    q, c = chip_of(me), me[3]
+    dp, tp = device_of(me)
+    src = q * 2 + c
     own = tp * 4 + dp
     cols = acc_ref.shape[1]
+    third = cols // 3
+    big = HALF[0]
     lanes = pl.ds(pl.multiple_of(q * cols, 128), cols)
     barrier = pltpu.get_barrier_semaphore()
     for d in range(NDEV):
@@ -177,62 +239,140 @@
             pl.semaphore_signal(barrier, inc=1, device_id=(d % 4, d // 4), device_id_type=MESH)
     pl.semaphore_wait(barrier, NDEV - 1)
 
+    def rows_on(d, core):
+        return pl.ds(pl.multiple_of(core * HALF[d], 8), HALF[d])
+
     def remote(d):
-        h = HALF[d]
         return pltpu.make_async_remote_copy(
-            src_ref=acc_ref.at[pl.ds(HBASE[d], h), :],
-            dst_ref=got_ref.at[pl.ds(pl.multiple_of(c * h, 8), h), lanes],
-            send_sem=send.at[d], recv_sem=recv.at[me],
+            src_ref=acc_ref.at[pl.ds(HBASE[d], HALF[d]), :], dst_ref=got_ref.at[rows_on(d, c), lanes],
+            send_sem=send.at[d], recv_sem=recv.at[src],
             device_id=(d % 4, d // 4), device_id_type=MESH)
 
     def local(d):
-        h = HALF[d]
         return pltpu.make_async_copy(
-            acc_ref.at[pl.ds(HBASE[d], h), :],
-            got_ref.at[pl.ds(pl.multiple_of(c * h, 8), h), lanes], lsem.at[0])
+            acc_ref.at[pl.ds(HBASE[d], HALF[d]), :], got_ref.at[rows_on(d, c), lanes], lsem.at[0])
+
+    def to_relay(chip, t, slot):
+        return pltpu.make_async_remote_copy(
+            src_ref=acc_ref.at[pl.ds(HBASE[0], big), pl.ds(t * third, third)], dst_ref=relay.at[slot],
+            send_sem=rsend.at[t], recv_sem=rrecv.at[slot],
+            device_id=(chip // 2, (chip % 2) * 2 + c), device_id_type=MESH)
+
+    def passed(slot, from_chip, t):
+        return pltpu.make_async_remote_copy(
+            src_ref=relay.at[slot],
+            dst_ref=got_ref.at[rows_on(0, c), pl.ds(from_chip * cols + t * third, third)],
+            send_sem=psend.at[slot], recv_sem=precv.at[(from_chip * 2 + c) * 3 + t],
+            device_id=(0, 0), device_id_type=MESH)
 
     wrow = acc_ref.at[pl.ds(HTOT, 8), :]
 
     def wcopy(k):
-        pdp, ptp, _ = peer(z, y, x, c, k)
         return pltpu.make_async_remote_copy(
             src_ref=wrow, dst_ref=w_ref.at[:, lanes],
             send_sem=wsend.at[k], recv_sem=wrecv.at[k],
-            device_id=(pdp, ptp), device_id_type=MESH)
-
+            device_id=device_of(flip(me, bits(k))), device_id_type=MESH)
+
+    direct0 = (q == 1) | (q == 2) | (q == 4) | (src == 1)
+    for chip, via in RELAYS.items():
+        @pl.when(q == chip)
+        def _():
+            for t in range(3):
+                to_relay(via, t, t).start()
+
+    @pl.when(q == 7)
+    def _():
+        for t in range(3):
+            to_relay(NEIGHBOURS[t], t, 3).start()
+
+    @pl.when(direct0)
+    def _():
+        remote(0).start()
+
+    @pl.when(own == 0)
+    def _():
+        local(0).start()
+
+    for d in range(1, NDEV):
+        @pl.when(own != d)
+        def _():
+            remote(d).start()
+
+        @pl.when(own == d)
+        def _():
+            local(d).start()
     for k in range(1, 8):
         wcopy(k).start()
     wlocal = pltpu.make_async_copy(wrow, w_ref.at[:, lanes], lsem.at[1])
     wlocal.start()
-    for d in range(NDEV):
-        @pl.when(own != d)
-        def _():
-            remote(d).start()
-
-        @pl.when(own == d)
-        def _():
-            local(d).start()
+
+    for i, chip in enumerate(NEIGHBOURS):
+        @pl.when(q == chip)
+        def _():
+            for slot in range(4):
+                to_relay(chip, 0, slot).wait_recv()
+                passed(slot, 7 if slot == 3 else RELAYED[chip], i if slot == 3 else slot).start()
+
     for k in range(1, 8):
         wcopy(k).wait()
     wlocal.wait()
+
+    def arrived(d, s):
+        h = HALF[d]
+        return pltpu.make_async_remote_copy(
+            src_ref=acc_ref.at[pl.ds(HBASE[d], h), :],
+            dst_ref=got_ref.at[pl.ds((s % 2) * h, h), pl.ds((s // 2) * cols, cols)],
+            send_sem=send.at[d], recv_sem=recv.at[s],
+            device_id=(0, 0), device_id_type=MESH)
+
+    def arrived_third(s, t):
+        return pltpu.make_async_remote_copy(
+            src_ref=relay.at[0],
+            dst_ref=got_ref.at[pl.ds((s % 2) * big, big), pl.ds((s // 2) * cols + t * third, third)],
+            send_sem=psend.at[0], recv_sem=precv.at[s * 3 + t],
+            device_id=(0, 0), device_id_type=MESH)
+
     for d in range(NDEV):
-        h = HALF[d]
-
         @pl.when(own == d)
         def _():
             local(d).wait()
             for s in range(NDEV):
-                @pl.when(me != s)
-                def _():
-                    pltpu.make_async_remote_copy(
-                        src_ref=acc_ref.at[pl.ds(HBASE[d], h), :],
-                        dst_ref=got_ref.at[pl.ds((s % 2) * h, h), pl.ds((s // 2) * cols, cols)],
-                        send_sem=send.at[d], recv_sem=recv.at[s],
-                        device_id=(s // 4, s % 4), device_id_type=MESH).wait_recv()
-
-        @pl.when(own != d)
-        def _():
-            remote(d).wait_send()
+                if d == 0 and s // 2 in (3, 5, 6, 7):
+                    for t in range(3):
+                        arrived_third(s, t).wait_recv()
+                elif d == 0:
+                    if s > 0:
+                        arrived(d, s).wait_recv()
+                else:
+                    @pl.when(src != s)
+                    def _():
+                        arrived(d, s).wait_recv()
+
+        if d > 0:
+            @pl.when(own != d)
+            def _():
+                remote(d).wait_send()
+
+    @pl.when(direct0)
+    def _():
+        remote(0).wait_send()
+
+    for chip, via in RELAYS.items():
+        @pl.when(q == chip)
+        def _():
+            for t in range(3):
+                to_relay(via, t, t).wait_send()
+
+    @pl.when(q == 7)
+    def _():
+        for t in range(3):
+            to_relay(NEIGHBOURS[t], t, 3).wait_send()
+
+    for i, chip in enumerate(NEIGHBOURS):
+        @pl.when(q == chip)
+        def _():
+            for slot in range(4):
+                passed(slot, 7 if slot == 3 else RELAYED[chip], i if slot == 3 else slot).wait_send()
 
 
 def send_to_owners(acc):
@@ -244,10 +384,15 @@
         in_specs=[pl.BlockSpec(memory_space=pltpu.VMEM)],
         out_specs=(pl.BlockSpec(memory_space=pl.ANY), pl.BlockSpec(memory_space=pl.ANY)),
         scratch_shapes=[
+            pltpu.VMEM((4, HALF[0], cols // 3), jnp.float32),
             pltpu.SemaphoreType.DMA((NDEV,)),
             pltpu.SemaphoreType.DMA((NDEV,)),
             pltpu.SemaphoreType.DMA((8,)),
             pltpu.SemaphoreType.DMA((8,)),
+            pltpu.SemaphoreType.DMA((4,)),
+            pltpu.SemaphoreType.DMA((NDEV * 3,)),
+            pltpu.SemaphoreType.DMA((3,)),
+            pltpu.SemaphoreType.DMA((4,)),
             pltpu.SemaphoreType.DMA((2,)),
         ],
         compiler_params=pltpu.CompilerParams(collective_id=2, has_side_effects=True),
@@ -295,8 +440,8 @@
     )(bounds, ids, got)
 
 
-def norm_kernel(c_ref, slots_ref, near_ref, mine0, mine1, theirs0, theirs1, dyn_ref, dyr_ref, w_ref,
-                x_ref, y_ref, g_ref, far, picked, wacc, sems):
+def norm_kernel(c_ref, slots_ref, own0, own1, theirs0, theirs1, mine_a, mine_b, his_a, his_b,
+                dyn_ref, dyr_ref, w_ref, x_ref, y_ref, g_ref, far, picked, wacc, sems):
     t = pl.program_id(0)
     last = pl.num_programs(0) - 1
     half = FAR_CAP // 2
@@ -306,9 +451,10 @@
     def _():
         wacc[...] = jnp.zeros_like(wacc)
         copies = []
-        for j, (ref, core) in enumerate(((mine0, c_ref[0]), (mine1, c_ref[0]), (theirs0, 1 - c_ref[0]), (theirs1, 1 - c_ref[0]))):
-            at = pl.multiple_of(core * half + (j % 2) * (half // 2), 8)
-            copies.append(pltpu.make_async_copy(ref, far.at[pl.ds(at, half // 2), :], sems.at[j]))
+        for j, ref in enumerate((mine_a, mine_b, his_a, his_b)):
+            core = c_ref[0] if j < 2 else 1 - c_ref[0]
+            at = pl.multiple_of(core * half + (j % 2) * FAR_CHUNKS[0], 8)
+            copies.append(pltpu.make_async_copy(ref, far.at[pl.ds(at, FAR_CHUNKS[j % 2]), :], sems.at[j]))
         for cp in copies:
             cp.start()
         far[pl.ds(FAR_CAP, 8), :] = jnp.zeros((8, width), jnp.float32)
@@ -318,30 +464,39 @@
     @pl.when(t < last)
     def _():
         def pick(i, carry):
-            rows = [far[pl.ds(slots_ref[t * ROW_TILE + i * 4 + u], 1), :] for u in range(4)]
-            for u in range(4):
-                picked[pl.ds(i * 4 + u, 1), :] = rows[u]
+            rows = [far[pl.ds(slots_ref[t * ROW_TILE + i * 8 + u], 1), :] for u in range(8)]
+            for u in range(8):
+                picked[pl.ds(i * 8 + u, 1), :] = rows[u]
             return carry
 
-        lax.fori_loop(0, ROW_TILE // 4, pick, 0)
+        lax.fori_loop(0, ROW_TILE // 8, pick, 0)
         gain = 1.0 + w_ref[...]
 
-        def body(i, carry):
-            at = pl.ds(pl.multiple_of(i * 16, 16), 16)
-            xb = (near_ref[at, :] + picked[at, :]).astype(jnp.bfloat16)
-            x_ref[at, :] = xb
-            xf = xb.astype(jnp.float32)
-            r = lax.rsqrt(jnp.sum(xf * xf, axis=1, keepdims=True) * (1.0 / width) + NORM_EPS)
-            xh = xf * r
-            y_ref[at, :] = (xh * gain).astype(jnp.bfloat16)
-            dy = dyn_ref[at, :].astype(jnp.float32)
-            wacc[...] += dy * xh
-            a = dy * gain
-            m = jnp.sum(a * xh, axis=1, keepdims=True) * (1.0 / width)
-            g_ref[at, :] = dyr_ref[at, :].astype(jnp.float32) + r * (a - xh * m)
-            return carry
-
-        lax.fori_loop(0, ROW_TILE // 16, body, 0)
+        def piece(own, theirs):
+            def body(i, carry):
+                at = pl.ds(pl.multiple_of(i * 16, 16), 16)
+                xb = (own[at, :] + theirs[at, :] + picked[at, :]).astype(jnp.bfloat16)
+                x_ref[at, :] = xb
+                xf = xb.astype(jnp.float32)
+                r = lax.rsqrt(jnp.sum(xf * xf, axis=1, keepdims=True) * (1.0 / width) + NORM_EPS)
+                xh = xf * r
+                y_ref[at, :] = (xh * gain).astype(jnp.bfloat16)
+                dy = dyn_ref[at, :].astype(jnp.float32)
+                wacc[...] += dy * xh
+                a = dy * gain
+                m = jnp.sum(a * xh, axis=1, keepdims=True) * (1.0 / width)
+                g_ref[at, :] = dyr_ref[at, :].astype(jnp.float32) + r * (a - xh * m)
+                return carry
+
+            lax.fori_loop(0, ROW_TILE // 16, body, 0)
+
+        @pl.when(t < NEAR_PIECE // ROW_TILE)
+        def _():
+            piece(own0, theirs0)
+
+        @pl.when(t >= NEAR_PIECE // ROW_TILE)
+        def _():
+            piece(own1, theirs1)
 
     @pl.when(t == last)
     def _():
@@ -350,16 +505,19 @@
         g_ref[pl.ds(0, 8), :] = jnp.where(first, total, 0.0)
 
 
-def norm(core, slots, near, far, dyn, dyr, w):
-    rows, width = near.shape
+def norm(core, slots, own, theirs, far, dyn, dyr, w):
+    rows, width = dyn.shape
     tiles = rows // ROW_TILE
+    per = NEAR_PIECE // ROW_TILE
     row = pl.BlockSpec((ROW_TILE, width), lambda i, *_: (jnp.minimum(i, tiles - 1), 0))
+    lower = pl.BlockSpec((ROW_TILE, width), lambda i, *_: (jnp.minimum(i, per - 1), 0))
+    upper = pl.BlockSpec((ROW_TILE, width), lambda i, *_: (jnp.clip(i - per, 0, per - 1), 0))
     anyspec = pl.BlockSpec(memory_space=pl.ANY)
     return pl.pallas_call(
         norm_kernel,
         grid_spec=pltpu.PrefetchScalarGridSpec(
             num_scalar_prefetch=2, grid=(tiles + 1,),
-            in_specs=[row] + [anyspec] * 4 + [row, row, pl.BlockSpec((1, width), lambda i, *_: (0, 0))],
+            in_specs=[lower, upper] * 2 + [anyspec] * 4 + [row, row, pl.BlockSpec((1, width), lambda i, *_: (0, 0))],
             out_specs=[row, row, pl.BlockSpec((ROW_TILE, width), lambda i, *_: (i, 0))],
             scratch_shapes=[
                 pltpu.VMEM((FAR_CAP + 8, width), jnp.float32),
@@ -373,7 +531,7 @@
                    jax.ShapeDtypeStruct((rows + 8, width), jnp.float32)),
         compiler_params=pltpu.CompilerParams(vmem_limit_bytes=60 * 2**20),
         name="assemble_norm",
-    )(core, slots, near, *far, dyn, dyr, w)
+    )(core, slots, *own, *theirs, *far, dyn, dyr, w)
 
 
 def solution(mesh):
@@ -440,11 +598,16 @@
         swap_core = [(t, t ^ 1) for t in range(4)]
         swap_x = [(t, t ^ 2) for t in range(4)]
 
-        def fetch(ids):
+        def raw(ids):
             ids = ids - tp * shard_rows
             owned = (ids >= 0) & (ids < shard_rows)
-            got = jnp.take(emb_table, jnp.where(owned, ids, 0), axis=0, mode="clip")
-            return jnp.where(owned[:, None], got.astype(jnp.float32) * scale_float, 0.0)
+            return jnp.take(emb_table, jnp.where(owned, ids, 0), axis=0, mode="clip"), owned[:, None]
+
+        def scaled(got, owned):
+            return jnp.where(owned, got.astype(jnp.float32) * scale_float, 0.0)
+
+        def fetch(ids):
+            return scaled(*raw(ids))
 
         def positions(toks, px, pc):
             return lax.dynamic_slice(toks, ((px * 2 + pc) * part,), (part,))
@@ -452,25 +615,30 @@
         listed, slots = far_lists(tokens.reshape(2, seq // 2))
         my_list = jnp.where(x == 0, listed[1], listed[0])
         my_slots = lax.dynamic_slice(slots.reshape(-1), (tp * part,), (part,))
-        half, n = FAR_CAP // 2, FAR_CAP // 2 // FWD_CHUNKS
+        half, at = FAR_CAP // 2, 0
         got, toks = [], tokens[0]
-        for k in range(FWD_CHUNKS):
-            theirs = lax.dynamic_slice(my_list, ((1 - c) * half + k * n,), (n,))
-            mine = lax.dynamic_slice(my_list, (c * half + k * n,), (n,))
-            both = fetch(theirs)
-            both = lax.ppermute(both, "tp", swap_core)
-            both = both + fetch(mine)
+        for n in FAR_CHUNKS:
+            theirs = lax.dynamic_slice(my_list, ((1 - c) * half + at,), (n,))
+            mine = lax.dynamic_slice(my_list, (c * half + at,), (n,))
+            at += n
+            pair, mask = lax.optimization_barrier(raw(jnp.concatenate([theirs, mine])))
+            both = lax.ppermute(scaled(pair[:n], mask[:n]), "tp", swap_core) + scaled(pair[n:], mask[n:])
             both, my_list, toks = lax.optimization_barrier((both, my_list, toks))
             got.append(lax.ppermute(both, "tp", swap_x))
         relayed = [lax.ppermute(r, "tp", swap_core) for r in got]
+        near_own, near_theirs = [], []
+        for k in range(part // NEAR_PIECE):
+            theirs = fetch(positions(toks, x, 1 - c)[k * NEAR_PIECE:(k + 1) * NEAR_PIECE])
+            near_theirs.append(lax.ppermute(theirs, "tp", swap_core))
         all_ids = lax.all_gather(toks[None], "dp", axis=0, tiled=True).reshape(-1)
-        near = fetch(positions(toks, x, 1 - c))
-        near = lax.ppermute(near, "tp", swap_core)
-        near = near + fetch(positions(toks, x, c))
+        for k in range(part // NEAR_PIECE):
+            near_own.append(fetch(positions(toks, x, c)[k * NEAR_PIECE:(k + 1) * NEAR_PIECE]))
+        near_own = lax.optimization_barrier(near_own)
         rows = part + 8
         overflow, work, count, my_ids, bounds = plan(all_ids, rows)
 
-        def dense_forward(near, toks):
+        def dense_forward(near_own, near_theirs, toks):
+            near = jnp.concatenate(near_own, axis=0) + jnp.concatenate(near_theirs, axis=0)
             far = lax.ppermute(fetch(positions(toks, 1 - x, 1 - c)), "tp", swap_core) + fetch(positions(toks, 1 - x, c))
             x_emb = (near + lax.ppermute(far, "tp", swap_x)).astype(jnp.bfloat16)
             x_float = x_emb.astype(jnp.float32)
@@ -484,11 +652,11 @@
             w_part = jnp.sum(dy_float * x_hat, axis=0)
             return x_emb, y_norm, jnp.concatenate([tok_grad, jnp.pad(w_part[None], ((0, 7), (0, 0)))], axis=0)
 
-        def sparse_forward(near, toks):
+        def sparse_forward(near_own, near_theirs, toks):
             core = c.astype(jnp.int32).reshape(1)
-            return tuple(norm(core, my_slots, near, got + relayed, dy_norm[0], dy_resid[0], w_norm[None]))
-
-        x_emb, y_norm, g_ext = lax.cond(overflow, dense_forward, sparse_forward, near, toks)
+            return tuple(norm(core, my_slots, near_own, near_theirs, got + relayed, dy_norm[0], dy_resid[0], w_norm[None]))
+
+        x_emb, y_norm, g_ext = lax.cond(overflow, dense_forward, sparse_forward, near_own, near_theirs, toks)
 
         cols = exchange_columns(g_ext)
         acc = sum_duplicates(work, count, cols, part)

time: 561 us -> 496 us (0.88)
  Pallas kernels: 315 us -> 280 us
  waiting for transfers between devices: 68.5 us -> 48 us
  local copies, waits for them, and re-layouts: 84.8 us -> 71.3 us
  starting transfers between devices: 19.2 us -> 25 us
    pallas_call x1, Pallas kernels: 108 us -> 81.7 us  [exchange_columns(): pl.pallas_call(columns_kernel, out_shape=jax.ShapeDtypeStruct((NDEV, rows...]
    ppermute x2, waiting for transfers between devices: 68.5 us -> 44.8 us  [local_step(): got.append(lax.ppermute(both, 'tp', swap_x))]
    gather x6, local copies, waits for them, and re-layouts: 81.9 us -> 68 us  [raw(): jnp.take(emb_table, jnp.where(owned, ids, 0), axis=0, mode='clip')]
    pallas_call x1, Pallas kernels: 124 us -> 114 us  [send_to_owners(): pl.pallas_call(owners_kernel, out_shape=(jax.ShapeDtypeStruct((CAPMAX, co...]
    add x3 -> x2, other arithmetic: 12.8 us -> 6.37 us  [local_step(): lax.ppermute(scaled(pair[:n], mask[:n]), 'tp', swap_core)]
    select_n x7 -> x9, other arithmetic: 5.68 us -> 11.9 us  [the longest x6 11.8 us: scaled(): return jnp.where(owned, got.astype(jnp.float32) * scale_float, 0.0)]
    ppermute x3 -> x4, starting transfers between devices: 12.4 us -> 15.4 us  [the longest x2 12.1 us: local_step(): lax.ppermute(scaled(pair[:n], mask[:n]), 'tp', swap_core)]
  transfers between devices with their start and end apart: 7 -> 8, of which waited for: 2 -> 3; matrix products, arithmetic and copies ran while one was open for 15% -> 17% of each run, Pallas kernels for 0% -> 0%
where the time goes in v1:
time: 496 us; the launch traced here: 487 us
  Pallas kernels  280 us (56%)
  local copies, waits for them, and re-layouts  71.3 us (14%)
  other arithmetic  48.5 us (10%)
  waiting for transfers between devices  48 us (10%)
  starting transfers between devices  25 us (5%)
  blocking collectives  8.35 us (2%)
    pallas_call x1, Pallas kernels, send_to_owners(): pl.pallas_call(owners_kernel, out_shape=(jax.ShapeDtypeStruct((CAPMAX, co...  114 us
    pallas_call x1, Pallas kernels, exchange_columns(): pl.pallas_call(columns_kernel, out_shape=jax.ShapeDtypeStruct((NDEV, rows...  81.7 us
    gather x6, local copies, waits for them, and re-layouts, raw(): jnp.take(emb_table, jnp.where(owned, ids, 0), axis=0, mode='clip')  68 us
    ppermute x2, waiting for transfers between devices, local_step(): got.append(lax.ppermute(both, 'tp', swap_x))  44.8 us
    pallas_call x1, Pallas kernels, expand(): pl.pallas_call(functools.partial(expand_kernel, scale), grid_spec=pltpu.P...  34.6 us
    pallas_call x1, Pallas kernels, sum_duplicates(): pl.pallas_call(functools.partial(sum_kernel, rows, tok_rows), grid_spec=p...  28.3 us
    pallas_call x1, Pallas kernels, norm(): pl.pallas_call(norm_kernel, grid_spec=pltpu.PrefetchScalarGridSpec(num_sc...  21.7 us
    ppermute x2, starting transfers between devices, local_step(): lax.ppermute(scaled(pair[:n], mask[:n]), 'tp', swap_core)  12.1 us
  transfers between devices with their start and end apart: 8, of which 3 were waited for; matrix products, arithmetic and copies ran while one was open for 17% of the time, Pallas kernels for 0%

profile of v1, /device:TPU:0, one launch (start us, length us, event | category | flops | bytes accessed | tf_op | source)
XLA Modules:
  0.0 487.0 jit_solution(3781190016696591305)
XLA Ops:
  3.9 1.8 select_reduce_fusion
  7.4 6.0 %gather_fusion.2 = bf16[256,3072]{1,0:T(8,128)(2,1)S(1)} fusion(bf16[16384,3072]{1,0:T(8,128)(2,1)} %param.13, s32[1024]{0:T(1024)S(1)} %pad_clamp_fusion.7), kind=kCustom, calls=%fused_computation.2 | custom fusion | bytes 3146752 | tf_op jit(solution)/shard_map/jit(_take)/gather | solution.py:604
  13.6 6.3 %collective-permute-start.8 = (f32[128,3072]{1,0:T(8,128)S(1)}, f32[128,3072]{1,0:T(8,128)}, u32[]{:S(2)}, u32[]{:S(2)}) collective-permute-start(f32[128,3072]{1,0:T(8,128)S(1)} %multiply_select_fusion.6), channel_id=1, source_target_pairs={{0,1},{1,0},{2,3},{3,2},{4,5},{5,4},{6,7},{7,6},{8,9},{9,8},{10,11... | collective-permute-start | bytes 4718600 | tf_op jit(solution)/shard_map/ppermute | solution.py:625
  19.9 3.2 collective-permute-done.8
  23.1 2.8 select_add_fusion.2
  26.1 14.7 %gather_fusion.3 = bf16[384,3072]{1,0:T(8,128)(2,1)S(1)} fusion(bf16[16384,3072]{1,0:T(8,128)(2,1)} %param.13, s32[1024]{0:T(1024)S(1)} %pad_clamp_fusion.6), kind=kCustom, calls=%fused_computation.3 | custom fusion | bytes 4720128 | tf_op jit(solution)/shard_map/jit(_take)/gather | solution.py:604
  42.7 5.8 %collective-permute-start.9 = (f32[192,3072]{1,0:T(8,128)}, f32[192,3072]{1,0:T(8,128)}, u32[]{:S(2)}, u32[]{:S(2)}) collective-permute-start(f32[192,3072]{1,0:T(8,128)} %multiply_select_fusion.5), channel_id=1, source_target_pairs={{0,1},{1,0},{2,3},{3,2},{4,5},{5,4},{6,7},{7,6},{8,9},{9,8},{10,11... | collective-permute-start | bytes 7077896 | tf_op jit(solution)/shard_map/ppermute | solution.py:625
  48.5 3.8 collective-permute-start.12
  52.3 35.2 %collective-permute-done.12 = f32[128,3072]{1,0:T(8,128)} collective-permute-done((f32[128,3072]{1,0:T(8,128)}, f32[128,3072]{1,0:T(8,128)}, u32[]{:S(2)}, u32[]{:S(2)}) %collective-permute-start.12) | collective-permute-done | bytes 1572896 | tf_op jit(solution)/shard_map/ppermute | solution.py:627
  87.5 3.5 select_add_fusion.1
  91.0 8.3 %all-gather = s32[8192]{0:T(1024)S(1)} all-gather(s32[2048]{0:T(1024)S(1)} %bitcast.55), channel_id=2, replica_groups=mesh['dp'=4,'tp'=4] {'dp'}, dimensions={0}, use_global_device_ids=true | all-gather | bytes 40960 | tf_op jit(solution)/shard_map/all_gather | solution.py:633
  99.5 5.6 %sort.21 = s32[8192]{0:T(1024)S(1)} sort(s32[8192]{0:T(1024)S(1)} %multiply_add_fusion), dimensions={0}, to_apply=%region_3.4 | sort | flops 106496 | bytes 65536 | tf_op jit(solution)/shard_map/sort | solution.py:542
  105.1 8.0 %gather_fusion.7 = bf16[256,3072]{1,0:T(8,128)(2,1)S(1)} fusion(bf16[16384,3072]{1,0:T(8,128)(2,1)} %param.13, s32[1024]{0:T(1024)S(1)} %pad_clamp_fusion.2), kind=kCustom, calls=%fused_computation.7 | custom fusion | bytes 3146752 | tf_op jit(solution)/shard_map/jit(_take)/gather | solution.py:604
  113.1 5.8 %collective-permute-start.13 = (f32[192,3072]{1,0:T(8,128)}, f32[192,3072]{1,0:T(8,128)}, u32[]{:S(2)}, u32[]{:S(2)}) collective-permute-start(f32[192,3072]{1,0:T(8,128)} %select_add_fusion.1), channel_id=1, source_target_pairs={{0,2},{1,3},{2,0},{3,1},{4,6},{5,7},{6,4},{7,5},{8,10},{9,11},{10,... | collective-permute-start | bytes 7077896 | tf_op jit(solution)/shard_map/ppermute | solution.py:627
  118.9 2.1 multiply_select_fusion.1
  121.7 7.4 %gather_fusion.6 = bf16[256,3072]{1,0:T(8,128)(2,1)S(1)} fusion(bf16[16384,3072]{1,0:T(8,128)(2,1)} %param.13, s32[1024]{0:T(1024)S(1)} %pad_clamp_fusion.3), kind=kCustom, calls=%fused_computation.6 | custom fusion | bytes 3146752 | tf_op jit(solution)/shard_map/jit(_take)/gather | solution.py:604
  129.1 3.2 collective-permute-start.11
  132.3 2.1 multiply_select_fusion.2
  135.6 23.0 %gather_fusion.5 = bf16[256,3072]{1,0:T(8,128)(2,1)S(1)} fusion(bf16[16384,3072]{1,0:T(8,128)(2,1)} %param.13, s32[1024]{0:T(1024)S(1)} %pad_clamp_fusion.4), kind=kCustom, calls=%fused_computation.5 | custom fusion | bytes 3146752 | tf_op jit(solution)/shard_map/jit(_take)/gather | solution.py:604
  159.9 9.6 %collective-permute-done.13 = f32[192,3072]{1,0:T(8,128)} collective-permute-done((f32[192,3072]{1,0:T(8,128)}, f32[192,3072]{1,0:T(8,128)}, u32[]{:S(2)}, u32[]{:S(2)}) %collective-permute-start.13) | collective-permute-done | bytes 2359328 | tf_op jit(solution)/shard_map/ppermute | solution.py:627
  169.6 2.1 multiply_select_fusion.3
  174.3 6.2 %sort.23.work_ref = s32[8192]{0:T(1024)} sort(s32[8192]{0:T(1024)S(1)} %get-tuple-element.230), dimensions={0}, to_apply=%region_21.22 | sort | flops 106496 | bytes 65536 | tf_op jit(solution)/shard_map/sort | solution.py:565
  180.5 5.6 %sort.22 = s32[8192]{0:T(1024)S(1)} sort(s32[8192]{0:T(1024)S(1)} %get-tuple-element.231), dimensions={0}, to_apply=%region_16.17 | sort | flops 106496 | bytes 65536 | tf_op jit(solution)/shard_map/sort | solution.py:567
  186.1 8.9 %gather_fusion.4 = bf16[256,3072]{1,0:T(8,128)(2,1)} fusion(bf16[16384,3072]{1,0:T(8,128)(2,1)} %param.13, s32[1024]{0:T(1024)S(1)} %pad_clamp_fusion.5), kind=kCustom, calls=%fused_computation.4 | custom fusion | bytes 3146752 | tf_op jit(solution)/shard_map/jit(_take)/gather | solution.py:604
  195.1 3.5 multiply_select_fusion.4
  200.5 22.8 %conditional.2 = (f32[520,3072]{1,0:T(8,128)}, bf16[512,3072]{1,0:T(8,128)(2,1)}, bf16[512,3072]{1,0:T(8,128)(2,1)}) conditional(s32[]{:T(128)} %convert_element_type.70, (s32[]{:T(128)}, s32[2048]{0:T(1024)S(1)}, s32[2,1024]{1,0:T(2,128)S(1)}, s32[2,1024]{1,0:T(2,128)S(1)}, s32[]{:T(128)}, /*index=5*/bf16[1,512,3072]{2,1,0:T(8,128)(2,1)S(1)}, ...), branch_computations={%region_8.9_spmd, %region_9.13_spmd} | conditional | flops 58277392 | bytes 198398368 | solution.py:659
  201.2 21.7 %assemble_norm.1 = (bf16[512,3072]{1,0:T(8,128)(2,1)}, bf16[512,3072]{1,0:T(8,128)(2,1)}, f32[520,3072]{1,0:T(8,128)}) custom-call(s32[1]{0:T(128)} %bitcast.c_ref, s32[512]{0:T(512)} %dynamic-slice_select_fusion.slots_ref, f32[256,3072]{1,0:T(8,128)} %get-tuple-element.120.own0, f32[256,3072]{1,0:T(8,128)} %get-tuple-element.121.own1, ...), custom_call_target="tpu_custom_call" | custom-call | tf_op jit(solution)/shard_map/cond/branch_0_fun/assemble_norm/pallas_call | solution.py:516
  223.3 81.7 %exchange_columns.1 = f32[16,520,384]{2,1,0:T(8,128)} custom-call(f32[520,3072]{1,0:T(8,128)} %get-tuple-element.187.g_ref), custom_call_target="tpu_custom_call" | custom-call | tf_op jit(solution)/shard_map/exchange_columns/pallas_call | solution.py:147
  305.0 28.3 %sum_duplicates.1.acc_ref = f32[2744,384]{1,0:T(8,128)} custom-call(s32[8192]{0:T(1024)} %sort.23.work_ref, s32[1]{0:T(128)} %bitcast.25.count_ref, f32[8320,384]{1,0:T(8,128)} %bitcast.51), custom_call_target="tpu_custom_call" | custom-call | tf_op jit(solution)/shard_map/sum_duplicates/pallas_call | solution.py:206
  333.3 113.6 %send_to_owners.1 = (f32[1536,3072]{1,0:T(8,128)}, f32[8,3072]{1,0:T(8,128)}) custom-call(f32[2744,384]{1,0:T(8,128)} %sum_duplicates.1.acc_ref), custom_call_target="tpu_custom_call" | custom-call | tf_op jit(solution)/shard_map/send_to_owners/pallas_call | solution.py:380
  448.4 37.5 %conditional.3 = (f32[4096,3072]{1,0:T(8,128)}) conditional(s32[]{:T(128)} %convert_element_type.70, (s32[8192]{0:T(1024)S(1)}, s32[]{:T(128)}, s32[35]{0:T(128)S(1)}, f32[1536,3072]{1,0:T(8,128)}) %tuple.44, (s32[]{:T(128)}, s32[1,2048]{1,0:T(1,128)S(1)}, f32[520,3072]{1,0:T(8,128)}, s32[]{:T(128)}) %tuple.96), branch_computations={%region_23.24_spmd, %region_24.26_spmd} | conditional | flops 94382144 | bytes 2019975552 | solution.py:683
  451.2 34.6 %expand.1 = f32[4096,3072]{1,0:T(8,128)} custom-call(s32[35]{0:T(128)S(1)} %get-tuple-element.146.bounds_ref, s32[1536]{0:T(1024)} %pad_dynamic-slice_fusion.ids_ref, f32[1536,3072]{1,0:T(8,128)} %get-tuple-element.149.got_ref), custom_call_target="tpu_custom_call" | custom-call | tf_op jit(solution)/shard_map/cond/branch_0_fun/expand/pallas_call | solution.py:430
  (70 shorter events, 16.4 us)
Async XLA Ops:
  13.6 9.4 %collective-permute-start.8 = (f32[128,3072]{1,0:T(8,128)S(1)}, f32[128,3072]{1,0:T(8,128)}, u32[]{:S(2)}, u32[]{:S(2)}) collective-permute-start(f32[128,3072]{1,0:T(8,128)S(1)} %multiply_select_fusion.6), channel_id=1, source_target_pairs={{0,1},{1,0},{2,3},{3,2},{4,5},{5,4},{6,7},{7,6},{8,9},{9,8},{10,11... | collective-permute-start | bytes 4718600 | tf_op jit(solution)/shard_map/ppermute | solution.py:625
  40.8 50.2 %copy-start.6 = (s32[1,2048]{1,0:T(1,128)S(1)}, s32[1,2048]{1,0:T(1,128)}, u32[]{:S(2)}) copy-start(s32[1,2048]{1,0:T(1,128)} %param.12) | copy-start | bytes 24580
  42.7 44.8 %collective-permute-start.9 = (f32[192,3072]{1,0:T(8,128)}, f32[192,3072]{1,0:T(8,128)}, u32[]{:S(2)}, u32[]{:S(2)}) collective-permute-start(f32[192,3072]{1,0:T(8,128)} %multiply_select_fusion.5), channel_id=1, source_target_pairs={{0,1},{1,0},{2,3},{3,2},{4,5},{5,4},{6,7},{7,6},{8,9},{9,8},{10,11... | collective-permute-start | bytes 7077896 | tf_op jit(solution)/shard_map/ppermute | solution.py:625
  48.5 39.0 %collective-permute-start.12 = (f32[128,3072]{1,0:T(8,128)}, f32[128,3072]{1,0:T(8,128)}, u32[]{:S(2)}, u32[]{:S(2)}) collective-permute-start(f32[128,3072]{1,0:T(8,128)} %select_add_fusion.2), channel_id=1, source_target_pairs={{0,2},{1,3},{2,0},{3,1},{4,6},{5,7},{6,4},{7,5},{8,10},{9,11},{10,... | collective-permute-start | bytes 4718600 | tf_op jit(solution)/shard_map/ppermute | solution.py:627
  87.5 113.0 %collective-permute-start.14 = (f32[128,3072]{1,0:T(8,128)}, f32[128,3072]{1,0:T(8,128)}, u32[]{:S(2)}, u32[]{:S(2)}) collective-permute-start(f32[128,3072]{1,0:T(8,128)} %collective-permute-done.12), channel_id=1, source_target_pairs={{0,1},{1,0},{2,3},{3,2},{4,5},{5,4},{6,7},{7,6},{8,9},{9,8},{10,11... | collective-permute-start | bytes 4718600 | tf_op jit(solution)/shard_map/ppermute | solution.py:628
  113.1 56.4 %collective-permute-start.13 = (f32[192,3072]{1,0:T(8,128)}, f32[192,3072]{1,0:T(8,128)}, u32[]{:S(2)}, u32[]{:S(2)}) collective-permute-start(f32[192,3072]{1,0:T(8,128)} %select_add_fusion.1), channel_id=1, source_target_pairs={{0,2},{1,3},{2,0},{3,1},{4,6},{5,7},{6,4},{7,5},{8,10},{9,11},{10,... | collective-permute-start | bytes 7077896 | tf_op jit(solution)/shard_map/ppermute | solution.py:627
  121.7 13.1 %copy-start.10 = (s32[16]{0:T(128)S(1)}, s32[16]{0:T(128)}, u32[]{:S(2)}) copy-start(s32[16]{0:T(128)} %constant.264.clone) | copy-start | bytes 196
  129.1 71.4 %collective-permute-start.11 = (f32[256,3072]{1,0:T(8,128)}, f32[256,3072]{1,0:T(8,128)}, u32[]{:S(2)}, u32[]{:S(2)}) collective-permute-start(f32[256,3072]{1,0:T(8,128)} %multiply_select_fusion.1), channel_id=1, source_target_pairs={{0,1},{1,0},{2,3},{3,2},{4,5},{5,4},{6,7},{7,6},{8,9},{9,8},{10,11... | collective-permute-start | bytes 9437192 | tf_op jit(solution)/shard_map/ppermute | solution.py:632
  134.4 66.0 %collective-permute-start.10 = (f32[256,3072]{1,0:T(8,128)}, f32[256,3072]{1,0:T(8,128)}, u32[]{:S(2)}, u32[]{:S(2)}) collective-permute-start(f32[256,3072]{1,0:T(8,128)} %multiply_select_fusion.2), channel_id=1, source_target_pairs={{0,1},{1,0},{2,3},{3,2},{4,5},{5,4},{6,7},{7,6},{8,9},{9,8},{10,11... | collective-permute-start | bytes 9437192 | tf_op jit(solution)/shard_map/ppermute | solution.py:632
  135.6 23.0 %copy-start.8 = (s32[16]{0:T(128)S(1)}, s32[16]{0:T(128)}, u32[]{:S(2)}) copy-start(s32[16]{0:T(128)} %constant.263.clone) | copy-start | bytes 196
  135.6 36.7 %copy-start.9 = (s32[16]{0:T(128)S(1)}, s32[16]{0:T(128)}, u32[]{:S(2)}) copy-start(s32[16]{0:T(128)} %constant.262.clone) | copy-start | bytes 196
  169.6 30.9 %collective-permute-start.15 = (f32[192,3072]{1,0:T(8,128)}, f32[192,3072]{1,0:T(8,128)}, u32[]{:S(2)}, u32[]{:S(2)}) collective-permute-start(f32[192,3072]{1,0:T(8,128)} %collective-permute-done.13), channel_id=1, source_target_pairs={{0,1},{1,0},{2,3},{3,2},{4,5},{5,4},{6,7},{7,6},{8,9},{9,8},{10,11... | collective-permute-start | bytes 7077896 | tf_op jit(solution)/shard_map/ppermute | solution.py:628
  186.1 14.4 %copy-start = (bf16[1,512,3072]{2,1,0:T(8,128)(2,1)S(1)}, bf16[1,512,3072]{2,1,0:T(8,128)(2,1)}, u32[]{:S(2)}) copy-start(bf16[1,512,3072]{2,1,0:T(8,128)(2,1)} %param.15) | copy-start | bytes 9437188
  186.1 14.4 %copy-start.7 = (f32[3072]{0:T(1024)S(1)}, f32[3072]{0:T(1024)}, u32[]{:S(2)}) copy-start(f32[3072]{0:T(1024)} %param.14) | copy-start | bytes 36868
